TPU v7x, 32 devices: a whole 2x2x4 slice. The times are simulated.
32 devices in a mesh: gx: 4 (over y, core), gy: 8 (over z, x).
Axes of the slice: x: 2, y: 2, z: 4, core: 2. Of those that a mesh axis runs over, the one named last changes fastest.
Arguments:
- forcing: float32 [16, 256, 1024], P(None, 'gy', 'gx'), may hold values from -6 to 6
- damping: float32 [16, 256, 1024], P(None, 'gy', 'gx'), may hold values from 0.5 to 4
- coupling: float32 [16, 16], replicated, may hold values from -1.5 to 1.5
- wind_lon: float32 [256, 1024], P('gy', 'gx'), may hold values from -0.5 to 0.5
- wind_lat: float32 [256, 1024], P('gy', 'gx'), may hold values from -0.5 to 0.5
Outputs:
- solution: float32 [16, 256, 1024], P(None, 'gy', 'gx')
- residual: float32 [16, 256, 1024], P(None, 'gy', 'gx')
All inputs are finite; a program needn't handle non-finite values.
Results may differ from a plain program's by a relative error of at most 0.0003.
Values sent between devices are 32-bit elements; how exact they have to be, the bound alone decides.
A program may use at most 64 MiB of HBM per device.

v0:
```python
import math

import jax
import jax.numpy as jnp
from jax import lax
from jax.sharding import PartitionSpec as P

ITERS = 8


COUPLE = 0.25
DIFF_LAT = 0.5
DIFF_LON = 0.5
GUARD = 1.0


def with_halo(cells, sides, width, closed):
    for axis, dim in sides:
        count = lax.axis_size(axis)
        ends = count if closed else count - 1
        head = lax.slice_in_dim(cells, 0, width, axis=dim)
        tail = lax.slice_in_dim(cells, cells.shape[dim] - width, cells.shape[dim], axis=dim)
        cells = jnp.concatenate(
            [
                lax.ppermute(tail, axis, [(i, (i + 1) % count) for i in range(ends)]),
                cells,
                lax.ppermute(head, axis, [((i + 1) % count, i) for i in range(ends)]),
            ],
            axis=dim,
        )
    return cells


def apply_core(padded, damping, coupling, wind_lon, wind_lat, diffuse_lon):
    centre = padded[:, 2:-2, 2:-2]
    east_one = padded[:, 2:-2, 3:-1]
    west_one = padded[:, 2:-2, 1:-3]
    east_two = padded[:, 2:-2, 4:]
    west_two = padded[:, 2:-2, :-4]
    north_one = padded[:, 3:-1, 2:-2]
    south_one = padded[:, 1:-3, 2:-2]
    north_two = padded[:, 4:, 2:-2]
    south_two = padded[:, :-4, 2:-2]
    slope_lon = (8.0 * (east_one - west_one) - (east_two - west_two)) / 12.0
    slope_lat = (8.0 * (north_one - south_one) - (north_two - south_two)) / 12.0
    coupled = COUPLE * jnp.einsum("ij,jab->iab", coupling, centre, precision=lax.Precision.HIGHEST)
    return (
        (1.0 + damping) * centre
        + coupled
        + diffuse_lon * (2.0 * centre - east_one - west_one)
        + DIFF_LAT * (2.0 * centre - north_one - south_one)
        + wind_lon * slope_lon
        + wind_lat * slope_lat
    )


def lon_diffusion(row_pos, lat_total):
    phi = -math.pi / 2 + (row_pos + 0.5) * (math.pi / lat_total)
    return DIFF_LON / (jnp.cos(phi) ** 2 + 0.1)


def least_squares(heights, first):
    num_steps = heights.shape[1]
    target = jnp.zeros((num_steps + 1,), jnp.float32).at[0].set(first)
    rotated = heights
    cosines = []
    sines = []
    for column in range(num_steps):
        column_vec = rotated[:, column]
        for earlier in range(column):
            upper_val = column_vec[earlier]
            lower_val = column_vec[earlier + 1]
            column_vec = column_vec.at[earlier].set(
                cosines[earlier] * upper_val + sines[earlier] * lower_val
            )
            column_vec = column_vec.at[earlier + 1].set(
                -sines[earlier] * upper_val + cosines[earlier] * lower_val
            )
        upper_val = column_vec[column]
        lower_val = column_vec[column + 1]
        radius = jnp.sqrt(upper_val * upper_val + lower_val * lower_val)
        cosine = upper_val / radius
        sine_val = lower_val / radius
        column_vec = column_vec.at[column].set(radius).at[column + 1].set(0.0)
        rotated = rotated.at[:, column].set(column_vec)
        upper_val = target[column]
        lower_val = target[column + 1]
        target = target.at[column].set(cosine * upper_val + sine_val * lower_val)
        target = target.at[column + 1].set(-sine_val * upper_val + cosine * lower_val)
        cosines.append(cosine)
        sines.append(sine_val)
    weights = [None] * num_steps
    for column in reversed(range(num_steps)):
        partial_value = target[column]
        for later_col in range(column + 1, num_steps):
            partial_value = partial_value - rotated[column, later_col] * weights[later_col]
        weights[column] = partial_value / rotated[column, column]
    return weights


def per_device(forcing, damping, coupling, wind_lon, wind_lat):
    channels, lat_rows, lon_cols = forcing.shape
    lat_total = lat_rows * lax.axis_size("gy")
    row_pos = (lax.axis_index("gy") * lat_rows + jnp.arange(lat_rows)).astype(jnp.float32)
    diffuse = lon_diffusion(row_pos, lat_total)[:, None]

    def matvec(source):
        padded = with_halo(source, (("gx", 2),), 2, True)
        padded = with_halo(padded, (("gy", 1),), 2, False)
        return (apply_core(padded, damping, coupling, wind_lon, wind_lat, diffuse), 0)

    initial = (forcing, 0)
    interior = initial[0]
    total_sq = lax.psum(jnp.sum(interior * interior), ("gx", "gy"))
    scale_first = jnp.sqrt(total_sq + GUARD)
    krylov = [(initial[0] / scale_first, initial[1])]
    heights = jnp.zeros((ITERS + 1, ITERS), jnp.float32)
    gram = (
        jnp.zeros((ITERS, ITERS), jnp.float32).at[0, 0].set(total_sq / (scale_first * scale_first))
    )
    for column in range(ITERS):
        applied, rim_new = matvec(krylov[column][0])
        applied_in = applied
        local_dots = jnp.stack([jnp.sum(vector * applied_in) for vector, rim_vec in krylov])
        count = len(krylov)
        coeffs, squared = lax.psum((local_dots, jnp.sum(applied_in * applied_in)), ("gx", "gy"))
        for earlier in range(count):
            applied = applied - coeffs[earlier] * krylov[earlier][0]
        gram_now = gram[:count, :count]
        gram_coef = jnp.sum(gram_now * coeffs[None, :], axis=1)
        norm_sq = jnp.maximum(
            squared - 2.0 * jnp.sum(coeffs * coeffs) + jnp.sum(coeffs * gram_coef), 0.0
        )
        subdiag = jnp.sqrt(norm_sq + GUARD)
        if column + 1 < ITERS:
            cross = (coeffs - gram_coef) / subdiag
            gram = gram.at[count, :count].set(cross).at[:count, count].set(cross)
            gram = gram.at[count, count].set(norm_sq / (subdiag * subdiag))
        heights = heights.at[: column + 1, column].set(coeffs).at[column + 1, column].set(subdiag)
        if column + 1 < ITERS:
            krylov.append((applied / subdiag, rim_new))
    weights = least_squares(heights, scale_first)
    solution = weights[0] * krylov[0][0]
    for column in range(1, ITERS):
        solution = solution + weights[column] * krylov[column][0]
    applied, rim_done = matvec(solution)
    residual = interior - applied
    return (solution, residual)


def solution(mesh):
    return jax.shard_map(
        per_device,
        mesh=mesh,
        in_specs=(P(None, "gy", "gx"), P(None, "gy", "gx"), P(), P("gy", "gx"), P("gy", "gx")),
        out_specs=(P(None, "gy", "gx"), P(None, "gy", "gx")),
        check_vma=False,
    )
```

profile of v0, /device:TPU:0, one launch (start us, length us, event | category | flops | bytes accessed | tf_op | source)
XLA Modules:
  0.0 827.5 jit_solution(9910483855664213307)
XLA Ops:
  2.5 42.2 %psum.119 = f32[]{:T(128)} all-reduce(f32[]{:T(128)} %multiply_reduce_fusion.44), channel_id=1, replica_groups=mesh['gx'=4,'gy'=8] {'gx','gy'}, use_global_device_ids=true, to_apply=%region_1.0 | all-reduce | flops 1 | bytes 8 | tf_op jit(solution)/shard_map/psum | solution.py:114
  56.6 4.5 collective-permute-start.3
  63.8 2.6 multiply_reduce_fusion.43
  66.4 42.0 %all-reduce.10 = (f32[]{:T(128)}, f32[1]{0:T(128)}) all-reduce(f32[]{:T(128)} %get-tuple-element.1667, f32[1]{0:T(128)} %bitcast.3), channel_id=1, replica_groups=mesh['gx'=4,'gy'=8] {'gx','gy'}, use_global_device_ids=true, to_apply=%region_5.0 | all-reduce | flops 2 | bytes 16 | tf_op jit(solution)/shard_map/psum | solution.py:126
  113.4 5.4 collective-permute-done.4
  118.8 3.3 collective-permute-done.5
  123.4 4.5 collective-permute-start.7
  141.2 3.2 multiply_reduce_fusion.41
  145.6 40.3 %all-reduce.9 = (f32[]{:T(128)}, f32[2]{0:T(128)S(1)}) all-reduce(f32[]{:T(128)} %get-tuple-element.1664, f32[2]{0:T(128)S(1)} %pad_maximum_fusion.54), channel_id=1, replica_groups=mesh['gx'=4,'gy'=8] {'gx','gy'}, use_global_device_ids=true, to_apply=%region_11.0 | all-reduce | flops 3 | bytes 24 | tf_op jit(solution)/shard_map/psum | solution.py:126
  189.2 2.7 subtract_divide_fusion.5
  195.1 3.4 collective-permute-done.8
  198.5 2.9 collective-permute-done.9
  202.8 4.5 collective-permute-start.11
  213.9 2.7 multiply_reduce_fusion.38
  218.6 39.5 %all-reduce.8 = (f32[]{:T(128)}, f32[3]{0:T(128)S(1)}) all-reduce(f32[]{:T(128)} %get-tuple-element.1660, f32[3]{0:T(128)S(1)} %pad_maximum_fusion.55), channel_id=1, replica_groups=mesh['gx'=4,'gy'=8] {'gx','gy'}, use_global_device_ids=true, to_apply=%region_21.0 | all-reduce | flops 4 | bytes 32 | tf_op jit(solution)/shard_map/psum | solution.py:126
  261.4 2.2 subtract_divide_fusion.4
  267.7 4.2 collective-permute-done.12
  275.4 4.5 collective-permute-start.15
  286.0 3.3 multiply_reduce_fusion.34
  289.2 2.6 pad_maximum_fusion.56
  291.9 40.2 %all-reduce.7 = (f32[]{:T(128)}, f32[4]{0:T(128)S(1)}) all-reduce(f32[]{:T(128)} %get-tuple-element.1655, f32[4]{0:T(128)S(1)} %pad_maximum_fusion.56), channel_id=1, replica_groups=mesh['gx'=4,'gy'=8] {'gx','gy'}, use_global_device_ids=true, to_apply=%region_32.0 | all-reduce | flops 5 | bytes 40 | tf_op jit(solution)/shard_map/psum | solution.py:126
  335.4 4.0 subtract_divide_fusion.3
  340.8 2.4 broadcast_select_fusion.16
  343.6 2.9 collective-permute-done.16
  346.5 3.4 collective-permute-done.17
  352.0 5.2 collective-permute-start.19
  357.8 2.5 broadcast_select_fusion.13
  367.1 4.4 multiply_reduce_fusion.25
  371.5 3.2 stack.147
  374.7 38.8 %all-reduce.6 = (f32[]{:T(128)}, f32[5]{0:T(128)S(1)}) all-reduce(f32[]{:T(128)} %get-tuple-element.1649, f32[5]{0:T(128)S(1)} %stack.147), channel_id=1, replica_groups=mesh['gx'=4,'gy'=8] {'gx','gy'}, use_global_device_ids=true, to_apply=%region_44.0 | all-reduce | flops 6 | bytes 48 | tf_op jit(solution)/shard_map/psum | solution.py:126
  416.8 4.7 subtract_divide_fusion.2
  423.2 2.5 broadcast_select_fusion.14
  426.0 3.1 collective-permute-done.20
  429.1 2.9 collective-permute-done.21
  434.1 5.2 collective-permute-start.23
  439.9 2.4 broadcast_select_fusion.11
  449.0 4.4 multiply_reduce_fusion.18
  453.4 3.8 stack.154
  457.2 39.7 %all-reduce.5 = (f32[]{:T(128)}, f32[6]{0:T(128)S(1)}) all-reduce(f32[]{:T(128)} %get-tuple-element.1642, f32[6]{0:T(128)S(1)} %stack.154), channel_id=1, replica_groups=mesh['gx'=4,'gy'=8] {'gx','gy'}, use_global_device_ids=true, to_apply=%region_57.0 | all-reduce | flops 7 | bytes 56 | tf_op jit(solution)/shard_map/psum | solution.py:126
  500.3 5.4 subtract_divide_fusion.1
  507.8 2.5 broadcast_select_fusion.12
  510.5 3.5 collective-permute-done.24
  514.0 2.6 collective-permute-done.25
  518.8 5.2 collective-permute-start.27
  524.6 2.4 broadcast_select_fusion.9
  531.5 2.1 pad_maximum_fusion.6
  534.2 4.4 multiply_reduce_fusion.10
  538.5 4.4 stack.162
  542.9 38.6 %all-reduce.4 = (f32[]{:T(128)}, f32[7]{0:T(128)S(1)}) all-reduce(f32[]{:T(128)} %get-tuple-element.1634, f32[7]{0:T(128)S(1)} %stack.162), channel_id=1, replica_groups=mesh['gx'=4,'gy'=8] {'gx','gy'}, use_global_device_ids=true, to_apply=%region_71.0 | all-reduce | flops 8 | bytes 64 | tf_op jit(solution)/shard_map/psum | solution.py:126
  584.7 6.3 subtract_divide_fusion
  592.9 2.4 broadcast_select_fusion.10
  595.5 3.4 collective-permute-done.28
  599.0 2.8 collective-permute-done.29
  603.9 5.2 collective-permute-start.31
  609.8 2.5 broadcast_select_fusion.7
  614.2 2.1 scatter.470
  616.7 2.1 pad_maximum_fusion.7
  619.4 3.6 multiply_reduce_fusion
  623.0 5.0 stack.171
  628.0 39.6 %all-reduce.3 = (f32[8]{0:T(128)S(1)}, f32[]{:T(128)}) all-reduce(f32[8]{0:T(128)S(1)} %stack.171, f32[]{:T(128)} %get-tuple-element.1624), channel_id=1, replica_groups=mesh['gx'=4,'gy'=8] {'gx','gy'}, use_global_device_ids=true, to_apply=%region_84.0 | all-reduce | flops 9 | bytes 72 | tf_op jit(solution)/shard_map/psum | solution.py:126
  806.9 5.7 collective-permute-done.32
  812.6 2.8 collective-permute-done.33
  816.9 4.5 collective-permute-start.35
  823.8 2.2 fusion.39
  (420 shorter events, 152.2 us)
Async XLA Ops:
  0.6 63.1 %copy-start = (f32[16,16]{1,0:T(8,128)S(1)}, f32[16,16]{1,0:T(8,128)}, u32[]{:S(2)}) copy-start(f32[16,16]{1,0:T(8,128)} %param.277) | copy-start | bytes 3076
  0.6 44.7 %copy-start.1 = (f32[16,32,256]{2,1,0:T(8,128)S(1)}, f32[16,32,256]{2,1,0:T(8,128)}, u32[]{:S(2)}) copy-start(f32[16,32,256]{2,1,0:T(8,128)} %param.275) | copy-start | bytes 1572868
  45.7 320.8 %copy-start.7 = (f32[16,32,256]{2,0,1:T(8,128)}, f32[16,32,256]{2,0,1:T(8,128)S(1)}, u32[]{:S(2)}) copy-start(f32[16,32,256]{2,0,1:T(8,128)S(1)} %copy_divide_fusion) | copy-start | bytes 1572868
  45.7 2.7 copy-start.46
  45.7 4.0 copy-start.45
  45.7 5.4 copy-start.44
  45.8 8.1 copy-start.12
  45.9 8.0 copy-start.11
  45.9 8.5 %collective-permute-start = (f32[16,32,2]{2,0,1:T(8,128)S(1)}, f32[16,32,2]{2,0,1:T(8,128)S(1)}, u32[]{:S(2)}, u32[]{:S(2)}) collective-permute-start(f32[16,32,2]{2,0,1:T(8,128)S(1)} %get-tuple-element.1751), channel_id=1, source_target_pairs={{8,0},{16,8},{24,16},{0,24},{9,1},{17,9},{25,17},{1,25},{10,2},{18... | collective-permute-start | bytes 12296 | tf_op jit(solution)/shard_map/ppermute | solution.py:27
  46.1 9.1 %collective-permute-start.1 = (f32[16,32,2]{2,0,1:T(8,128)S(1)}, f32[16,32,2]{2,0,1:T(8,128)S(1)}, u32[]{:S(2)}, u32[]{:S(2)}) collective-permute-start(f32[16,32,2]{2,0,1:T(8,128)S(1)} %get-tuple-element.1750), channel_id=1, source_target_pairs={{0,8},{8,16},{16,24},{24,0},{1,9},{9,17},{17,25},{25,1},{2,10},{10... | collective-permute-start | bytes 12296 | tf_op jit(solution)/shard_map/ppermute | solution.py:25
  53.9 231.7 %copy-start.13 = (f32[32,256]{1,0:T(8,128)}, f32[32,256]{1,0:T(8,128)S(1)}, u32[]{:S(2)}) copy-start(f32[32,256]{1,0:T(8,128)S(1)} %get-tuple-element.1865) | copy-start | bytes 98308
  55.3 6.6 collective-permute-start.2
  56.6 6.5 collective-permute-start.3
  61.2 224.3 %copy-start.37 = (f32[32]{0:T(128)}, f32[32]{0:T(128)S(1)}, u32[]{:S(2)}) copy-start(f32[32]{0:T(128)S(1)} %add_divide_fusion) | copy-start | bytes 388
  61.9 1.9 copy-start.28
  112.7 6.0 collective-permute-start.4
  113.4 8.6 %collective-permute-start.5 = (f32[16,32,2]{2,0,1:T(8,128)S(1)}, f32[16,32,2]{2,0,1:T(8,128)S(1)}, u32[]{:S(2)}, u32[]{:S(2)}) collective-permute-start(f32[16,32,2]{2,0,1:T(8,128)S(1)} %get-tuple-element.1748), channel_id=1, source_target_pairs={{0,8},{8,16},{16,24},{24,0},{1,9},{9,17},{17,25},{25,1},{2,10},{10... | collective-permute-start | bytes 12296 | tf_op jit(solution)/shard_map/ppermute | solution.py:25
  122.1 18.0 %collective-permute-start.6 = (f32[16,2,260]{2,0,1:T(8,128)S(1)}, f32[16,2,260]{2,0,1:T(8,128)S(1)}, u32[]{:S(2)}, u32[]{:S(2)}) collective-permute-start(f32[16,2,260]{2,0,1:T(8,128)S(1)} %get-tuple-element.1728), channel_id=1, source_target_pairs={{1,0},{2,1},{3,2},{4,3},{5,4},{6,5},{7,6},{9,8},{10,9},{11,10},{12... | collective-permute-start | bytes 99848 | tf_op jit(solution)/shard_map/ppermute | solution.py:27
  123.4 16.7 %collective-permute-start.7 = (f32[16,2,260]{2,0,1:T(8,128)S(1)}, f32[16,2,260]{2,0,1:T(8,128)S(1)}, u32[]{:S(2)}, u32[]{:S(2)}) collective-permute-start(f32[16,2,260]{2,0,1:T(8,128)S(1)} %get-tuple-element.1729), channel_id=1, source_target_pairs={{0,1},{1,2},{2,3},{3,4},{4,5},{5,6},{6,7},{8,9},{9,10},{10,11},{11... | collective-permute-start | bytes 99848 | tf_op jit(solution)/shard_map/ppermute | solution.py:25
  192.0 6.5 collective-permute-start.8
  192.9 8.4 %collective-permute-start.9 = (f32[16,32,2]{2,0,1:T(8,128)S(1)}, f32[16,32,2]{2,0,1:T(8,128)S(1)}, u32[]{:S(2)}, u32[]{:S(2)}) collective-permute-start(f32[16,32,2]{2,0,1:T(8,128)S(1)} %get-tuple-element.1746), channel_id=1, source_target_pairs={{0,8},{8,16},{16,24},{24,0},{1,9},{9,17},{17,25},{25,1},{2,10},{10... | collective-permute-start | bytes 12296 | tf_op jit(solution)/shard_map/ppermute | solution.py:25
  201.5 11.4 %collective-permute-start.10 = (f32[16,2,260]{2,0,1:T(8,128)S(1)}, f32[16,2,260]{2,0,1:T(8,128)S(1)}, u32[]{:S(2)}, u32[]{:S(2)}) collective-permute-start(f32[16,2,260]{2,0,1:T(8,128)S(1)} %get-tuple-element.1724), channel_id=1, source_target_pairs={{1,0},{2,1},{3,2},{4,3},{5,4},{6,5},{7,6},{9,8},{10,9},{11,10},{12... | collective-permute-start | bytes 99848 | tf_op jit(solution)/shard_map/ppermute | solution.py:27
  202.8 10.1 %collective-permute-start.11 = (f32[16,2,260]{2,0,1:T(8,128)S(1)}, f32[16,2,260]{2,0,1:T(8,128)S(1)}, u32[]{:S(2)}, u32[]{:S(2)}) collective-permute-start(f32[16,2,260]{2,0,1:T(8,128)S(1)} %get-tuple-element.1725), channel_id=1, source_target_pairs={{0,1},{1,2},{2,3},{3,4},{4,5},{5,6},{6,7},{8,9},{9,10},{10,11},{11... | collective-permute-start | bytes 99848 | tf_op jit(solution)/shard_map/ppermute | solution.py:25
  264.4 7.5 collective-permute-start.12
  265.5 8.5 %collective-permute-start.13 = (f32[16,32,2]{2,0,1:T(8,128)S(1)}, f32[16,32,2]{2,0,1:T(8,128)S(1)}, u32[]{:S(2)}, u32[]{:S(2)}) collective-permute-start(f32[16,32,2]{2,0,1:T(8,128)S(1)} %get-tuple-element.1744), channel_id=1, source_target_pairs={{0,8},{8,16},{16,24},{24,0},{1,9},{9,17},{17,25},{25,1},{2,10},{10... | collective-permute-start | bytes 12296 | tf_op jit(solution)/shard_map/ppermute | solution.py:25
  274.1 10.9 %collective-permute-start.14 = (f32[16,2,260]{2,0,1:T(8,128)S(1)}, f32[16,2,260]{2,0,1:T(8,128)S(1)}, u32[]{:S(2)}, u32[]{:S(2)}) collective-permute-start(f32[16,2,260]{2,0,1:T(8,128)S(1)} %get-tuple-element.1720), channel_id=1, source_target_pairs={{1,0},{2,1},{3,2},{4,3},{5,4},{6,5},{7,6},{9,8},{10,9},{11,10},{12... | collective-permute-start | bytes 99848 | tf_op jit(solution)/shard_map/ppermute | solution.py:27
  275.4 9.6 %collective-permute-start.15 = (f32[16,2,260]{2,0,1:T(8,128)S(1)}, f32[16,2,260]{2,0,1:T(8,128)S(1)}, u32[]{:S(2)}, u32[]{:S(2)}) collective-permute-start(f32[16,2,260]{2,0,1:T(8,128)S(1)} %get-tuple-element.1721), channel_id=1, source_target_pairs={{0,1},{1,2},{2,3},{3,4},{4,5},{5,6},{6,7},{8,9},{9,10},{10,11},{11... | collective-permute-start | bytes 99848 | tf_op jit(solution)/shard_map/ppermute | solution.py:25
  335.4 7.9 copy-start.26
  340.2 6.2 collective-permute-start.16
  340.8 9.0 %collective-permute-start.17 = (f32[16,32,2]{2,0,1:T(8,128)}, f32[16,32,2]{2,0,1:T(8,128)}, u32[]{:S(2)}, u32[]{:S(2)}) collective-permute-start(f32[16,32,2]{2,0,1:T(8,128)} %get-tuple-element.1742), channel_id=1, source_target_pairs={{0,8},{8,16},{16,24},{24,0},{1,9},{9,17},{17,25},{25,1},{2,10},{10... | collective-permute-start | bytes 12296 | tf_op jit(solution)/shard_map/ppermute | solution.py:25
  350.7 14.0 %collective-permute-start.18 = (f32[16,2,260]{2,0,1:T(8,128)S(1)}, f32[16,2,260]{2,0,1:T(8,128)}, u32[]{:S(2)}, u32[]{:S(2)}) collective-permute-start(f32[16,2,260]{2,0,1:T(8,128)S(1)} %get-tuple-element.1716), channel_id=1, source_target_pairs={{1,0},{2,1},{3,2},{4,3},{5,4},{6,5},{7,6},{9,8},{10,9},{11,10},{12... | collective-permute-start | bytes 99848 | tf_op jit(solution)/shard_map/ppermute | solution.py:27
  352.0 12.7 %collective-permute-start.19 = (f32[16,2,260]{2,0,1:T(8,128)S(1)}, f32[16,2,260]{2,0,1:T(8,128)}, u32[]{:S(2)}, u32[]{:S(2)}) collective-permute-start(f32[16,2,260]{2,0,1:T(8,128)S(1)} %get-tuple-element.1717), channel_id=1, source_target_pairs={{0,1},{1,2},{2,3},{3,4},{4,5},{5,6},{6,7},{8,9},{9,10},{10,11},{11... | collective-permute-start | bytes 99848 | tf_op jit(solution)/shard_map/ppermute | solution.py:25
  364.7 1.8 copy-start.14
  416.7 9.0 %copy-start.24 = (f32[5]{0:T(128)}, f32[5]{0:T(128)S(1)}, u32[]{:S(2)}) copy-start(f32[5]{0:T(128)S(1)} %subtract_divide_fusion.9) | copy-start | bytes 64
  422.4 6.7 collective-permute-start.20
  423.2 8.8 %collective-permute-start.21 = (f32[16,32,2]{2,0,1:T(8,128)}, f32[16,32,2]{2,0,1:T(8,128)}, u32[]{:S(2)}, u32[]{:S(2)}) collective-permute-start(f32[16,32,2]{2,0,1:T(8,128)} %get-tuple-element.1740), channel_id=1, source_target_pairs={{0,8},{8,16},{16,24},{24,0},{1,9},{9,17},{17,25},{25,1},{2,10},{10... | collective-permute-start | bytes 12296 | tf_op jit(solution)/shard_map/ppermute | solution.py:25
  432.8 13.9 %collective-permute-start.22 = (f32[16,2,260]{2,0,1:T(8,128)S(1)}, f32[16,2,260]{2,0,1:T(8,128)}, u32[]{:S(2)}, u32[]{:S(2)}) collective-permute-start(f32[16,2,260]{2,0,1:T(8,128)S(1)} %get-tuple-element.1712), channel_id=1, source_target_pairs={{1,0},{2,1},{3,2},{4,3},{5,4},{6,5},{7,6},{9,8},{10,9},{11,10},{12... | collective-permute-start | bytes 99848 | tf_op jit(solution)/shard_map/ppermute | solution.py:27
  434.1 12.6 %collective-permute-start.23 = (f32[16,2,260]{2,0,1:T(8,128)S(1)}, f32[16,2,260]{2,0,1:T(8,128)}, u32[]{:S(2)}, u32[]{:S(2)}) collective-permute-start(f32[16,2,260]{2,0,1:T(8,128)S(1)} %get-tuple-element.1713), channel_id=1, source_target_pairs={{0,1},{1,2},{2,3},{3,4},{4,5},{5,6},{6,7},{8,9},{9,10},{10,11},{11... | collective-permute-start | bytes 99848 | tf_op jit(solution)/shard_map/ppermute | solution.py:25
  446.6 1.8 copy-start.8
  446.6 1.8 copy-start.15
  446.6 1.8 copy-start.33
  500.3 10.0 %copy-start.22 = (f32[6]{0:T(128)}, f32[6]{0:T(128)S(1)}, u32[]{:S(2)}) copy-start(f32[6]{0:T(128)S(1)} %subtract_divide_fusion.8) | copy-start | bytes 76
  506.6 7.4 collective-permute-start.24
  507.8 8.8 %collective-permute-start.25 = (f32[16,32,2]{2,0,1:T(8,128)}, f32[16,32,2]{2,0,1:T(8,128)}, u32[]{:S(2)}, u32[]{:S(2)}) collective-permute-start(f32[16,32,2]{2,0,1:T(8,128)} %get-tuple-element.1738), channel_id=1, source_target_pairs={{0,8},{8,16},{16,24},{24,0},{1,9},{9,17},{17,25},{25,1},{2,10},{10... | collective-permute-start | bytes 12296 | tf_op jit(solution)/shard_map/ppermute | solution.py:25
  517.5 14.0 %collective-permute-start.26 = (f32[16,2,260]{2,0,1:T(8,128)S(1)}, f32[16,2,260]{2,0,1:T(8,128)}, u32[]{:S(2)}, u32[]{:S(2)}) collective-permute-start(f32[16,2,260]{2,0,1:T(8,128)S(1)} %get-tuple-element.1708), channel_id=1, source_target_pairs={{1,0},{2,1},{3,2},{4,3},{5,4},{6,5},{7,6},{9,8},{10,9},{11,10},{12... | collective-permute-start | bytes 99848 | tf_op jit(solution)/shard_map/ppermute | solution.py:27
  518.8 12.7 %collective-permute-start.27 = (f32[16,2,260]{2,0,1:T(8,128)S(1)}, f32[16,2,260]{2,0,1:T(8,128)}, u32[]{:S(2)}, u32[]{:S(2)}) collective-permute-start(f32[16,2,260]{2,0,1:T(8,128)S(1)} %get-tuple-element.1709), channel_id=1, source_target_pairs={{0,1},{1,2},{2,3},{3,4},{4,5},{5,6},{6,7},{8,9},{9,10},{10,11},{11... | collective-permute-start | bytes 99848 | tf_op jit(solution)/shard_map/ppermute | solution.py:25
  531.4 2.2 copy-start.3
  531.4 2.2 copy-start.9
  531.4 2.2 copy-start.16
  531.4 2.2 copy-start.34
  584.7 10.6 %copy-start.20 = (f32[7]{0:T(128)}, f32[7]{0:T(128)S(1)}, u32[]{:S(2)}) copy-start(f32[7]{0:T(128)S(1)} %subtract_divide_fusion.7) | copy-start | bytes 88
  592.0 7.0 collective-permute-start.28
  592.9 8.8 %collective-permute-start.29 = (f32[16,32,2]{2,0,1:T(8,128)}, f32[16,32,2]{2,0,1:T(8,128)}, u32[]{:S(2)}, u32[]{:S(2)}) collective-permute-start(f32[16,32,2]{2,0,1:T(8,128)} %get-tuple-element.1736), channel_id=1, source_target_pairs={{0,8},{8,16},{16,24},{24,0},{1,9},{9,17},{17,25},{25,1},{2,10},{10... | collective-permute-start | bytes 12296 | tf_op jit(solution)/shard_map/ppermute | solution.py:25
  602.6 14.0 %collective-permute-start.30 = (f32[16,2,260]{2,0,1:T(8,128)S(1)}, f32[16,2,260]{2,0,1:T(8,128)}, u32[]{:S(2)}, u32[]{:S(2)}) collective-permute-start(f32[16,2,260]{2,0,1:T(8,128)S(1)} %get-tuple-element.1704), channel_id=1, source_target_pairs={{1,0},{2,1},{3,2},{4,3},{5,4},{6,5},{7,6},{9,8},{10,9},{11,10},{12... | collective-permute-start | bytes 99848 | tf_op jit(solution)/shard_map/ppermute | solution.py:27
  603.9 12.7 %collective-permute-start.31 = (f32[16,2,260]{2,0,1:T(8,128)S(1)}, f32[16,2,260]{2,0,1:T(8,128)}, u32[]{:S(2)}, u32[]{:S(2)}) collective-permute-start(f32[16,2,260]{2,0,1:T(8,128)S(1)} %get-tuple-element.1705), channel_id=1, source_target_pairs={{0,1},{1,2},{2,3},{3,4},{4,5},{5,6},{6,7},{8,9},{9,10},{10,11},{11... | collective-permute-start | bytes 99848 | tf_op jit(solution)/shard_map/ppermute | solution.py:25
  616.6 2.2 copy-start.4
  616.6 2.2 copy-start.6
  616.6 2.2 copy-start.10
  616.6 2.2 copy-start.17
  616.6 2.2 copy-start.35
  805.8 6.8 collective-permute-start.32
  806.9 8.6 %collective-permute-start.33 = (f32[16,32,2]{2,0,1:T(8,128)S(1)}, f32[16,32,2]{2,0,1:T(8,128)S(1)}, u32[]{:S(2)}, u32[]{:S(2)}) collective-permute-start(f32[16,32,2]{2,0,1:T(8,128)S(1)} %get-tuple-element.1734), channel_id=1, source_target_pairs={{0,8},{8,16},{16,24},{24,0},{1,9},{9,17},{17,25},{25,1},{2,10},{10... | collective-permute-start | bytes 12296 | tf_op jit(solution)/shard_map/ppermute | solution.py:25
  815.6 7.0 collective-permute-start.34
  816.9 6.3 collective-permute-start.35
  (20 other events, 17.7 us)
where the time goes:
time: 842 us; the launch traced here: 828 us
  blocking collectives  361 us (43%)
  between operations  118 us (14%)
  local copies, waits for them, and re-layouts  99.7 us (12%)
  other arithmetic  98.6 us (12%)
  starting transfers between devices  62.8 us (7%)
  waiting for transfers between devices  57 us (7%)
  matrix products  30.6 us (4%)
    psum x8, blocking collectives, per_device(): lax.psum((local_dots, jnp.sum(applied_in * applied_in)), ('gx', 'gy'))  319 us
    ppermute x18, starting transfers between devices, with_halo(): lax.ppermute(tail, axis, [(i, (i + 1) % count) for i in range(ends)])  43.8 us
    another operation x38, other arithmetic  42.5 us
    psum x1, blocking collectives, per_device(): total_sq = lax.psum(jnp.sum(interior * interior), ('gx', 'gy'))  42.2 us
    ppermute x18, waiting for transfers between devices, with_halo(): lax.ppermute(head, axis, [((i + 1) % count, i) for i in range(ends)])  31.6 us
    dot_general x9, matrix products, apply_core(): jnp.einsum('ij,jab->iab', coupling, centre, precision=lax.Precision.HIGHEST)  30.6 us
    div x7, other arithmetic, per_device(): krylov.append((applied / subdiag, rim_new))  26.3 us
    ppermute x18, waiting for transfers between devices, with_halo(): lax.ppermute(tail, axis, [(i, (i + 1) % count) for i in range(ends)])  25.4 us
  transfers between devices with their start and end apart: 36, of which 19 were waited for; matrix products, arithmetic and copies ran while one was open for 9% of the time, Pallas kernels for 0%

commit v1 on v0

v1 whole, which is shorter than its diff:
```python
import functools
import math

import jax
import jax.numpy as jnp
from jax import lax
from jax.experimental import pallas as pl
from jax.experimental.pallas import tpu as pltpu
from jax.sharding import PartitionSpec as P

ITERS = 8
COUPLE = 0.25
DIFF_LAT = 0.5
DIFF_LON = 0.5
GUARD = 1.0
MESH = pl.DeviceIdType.MESH
HI = lax.Precision.HIGHEST

MIDDLE = 9.0
RADIUS = 6.0
WIDTH = 3.0
THETA = [MIDDLE + RADIUS * math.cos(math.pi * (2 * k + 1) / (2 * ITERS)) for k in (7, 0, 4, 2, 6, 1, 5, 3)]
PAIRS = [(k, i) for k in range(ITERS + 1) for i in range(k + 1)]
SLOTS = 48


def apply_to(coords):
    out = [None] * (len(coords) + 1)
    for k, value in enumerate(coords):
        low = THETA[k] * value if k < ITERS else value
        out[k] = low if out[k] is None else out[k] + low
        out[k + 1] = WIDTH * value
    return out


def small_solve(gram):
    first = jnp.sqrt(gram[0][0] + GUARD)
    coords = [[1.0 / first]]
    images = [[gram[i][0] * coords[0][0] for i in range(ITERS + 1)]]
    heights = []
    for j in range(ITERS):
        moved = apply_to(coords[j])
        column = []
        for i in range(j + 1):
            column.append(functools.reduce(lambda a, b: a + b, [images[i][k] * moved[k] for k in range(j + 2)]))
        left = list(moved)
        for i in range(j + 1):
            for k in range(i + 1):
                left[k] = left[k] - column[i] * coords[i][k]
        image = [
            functools.reduce(lambda a, b: a + b, [gram[r][k] * left[k] for k in range(j + 2)])
            for r in range(ITERS + 1)
        ]
        norm_sq = functools.reduce(lambda a, b: a + b, [image[k] * left[k] for k in range(j + 2)])
        subdiag = jnp.sqrt(jnp.maximum(norm_sq, 0.0) + GUARD)
        column.append(subdiag)
        heights.append(column)
        inverse = 1.0 / subdiag
        coords.append([v * inverse for v in left])
        images.append([v * inverse for v in image])
    cosines, sines, target, rotated = [], [], [first], []
    for j in range(ITERS):
        column = list(heights[j])
        for e in range(j):
            upper, lower = column[e], column[e + 1]
            column[e] = cosines[e] * upper + sines[e] * lower
            column[e + 1] = cosines[e] * lower - sines[e] * upper
        upper, lower = column[j], column[j + 1]
        radius = jnp.sqrt(upper * upper + lower * lower)
        inverse = 1.0 / radius
        cosine, sine = upper * inverse, lower * inverse
        column[j] = radius
        kept = target[j]
        target[j] = cosine * kept
        target.append(-sine * kept)
        cosines.append(cosine)
        sines.append(sine)
        rotated.append(column)
    weights = [None] * ITERS
    for j in reversed(range(ITERS)):
        value = target[j]
        for later in range(j + 1, ITERS):
            value = value - rotated[later][j] * weights[later]
        weights[j] = value / rotated[j][j]
    answer = [None] * ITERS
    for j in range(ITERS):
        for k in range(j + 1):
            term = weights[j] * coords[j][k]
            answer[k] = term if answer[k] is None else answer[k] + term
    return answer, apply_to(answer)


def kernel(nx, ny, f_hbm, d_hbm, c_ref, wl_ref, wa_ref, kx_ref, sol_hbm, res_hbm,
           basis, diag, coef, block, west_in, east_in, west_out, east_out, gram_acc, mine, slots, splats, outs,
           in_sem, out_sem, lat_send, lat_recv, lon_send, lon_recv, red_send, red_recv):
    channels, lat, lon = f_hbm.shape
    tiles = lon // 128
    total = nx * ny
    ix, iy = lax.axis_index("gx"), lax.axis_index("gy")
    me = ix * ny + iy
    east, west = lax.rem(ix + 1, nx), lax.rem(ix + nx - 1, nx)

    loads = []
    for c in range(channels):
        for q, (src, dst) in enumerate(((f_hbm, basis.at[0]), (d_hbm, diag))):
            off = 2 if q == 0 else 0
            copy = pltpu.make_async_copy(src.at[c], dst.at[pl.ds(off, lat), c, :], in_sem.at[q, c])
            copy.start()
            loads.append(copy)

    barrier = pltpu.get_barrier_semaphore()

    def greet(o, _):
        other = lax.rem(me + o, total)
        pl.semaphore_signal(barrier, inc=1, device_id=(other // ny, lax.rem(other, ny)), device_id_type=MESH)
        return 0

    lax.fori_loop(1, total, greet, 0)

    scale = 1.0 / WIDTH
    row = lax.broadcasted_iota(jnp.int32, (128, channels), 0)
    col = lax.broadcasted_iota(jnp.int32, (128, channels), 1)
    spread = jnp.where(lax.rem(row, channels) == col, 1.0, 0.0).astype(jnp.float32)
    wide = lax.dot_general(spread, c_ref[...], (((1,), (0,)), ((), ())), precision=HI,
                           preferred_element_type=jnp.float32)
    wide = lax.dot_general(wide, spread, (((1,), (1,)), ((), ())), precision=HI,
                           preferred_element_type=jnp.float32)
    same = (lax.broadcasted_iota(jnp.int32, (128, 128), 0) // channels
            == lax.broadcasted_iota(jnp.int32, (128, 128), 1) // channels)
    block[...] = jnp.where(same, wide * (COUPLE * scale), 0.0)
    kx = kx_ref[...] * scale
    wl = wl_ref[...] * (scale / 12.0)
    wa = wa_ref[...] * (scale / 12.0)
    coef[0] = 8.0 * wl - kx
    coef[1] = -8.0 * wl - kx
    coef[2] = wl
    coef[3] = 8.0 * wa - DIFF_LAT * scale
    coef[4] = -8.0 * wa - DIFF_LAT * scale
    coef[5] = wa
    coef[6] = 2.0 * kx + (1.0 + 2.0 * DIFF_LAT) * scale

    def clear(k, _):
        empty = jnp.zeros((2, channels, lon), jnp.float32)

        @pl.when(iy == 0)
        def _():
            basis[k, 0:2] = empty

        @pl.when(iy == ny - 1)
        def _():
            basis[k, lat + 2:lat + 4] = empty

        return 0

    lax.fori_loop(0, ITERS, clear, 0)

    for copy in loads:
        copy.wait()

    def prepare(b, _):
        extra = coef[6, pl.ds(pl.multiple_of(b * 8, 8), 8), :]
        for j in range(8):
            diag[b * 8 + j] = diag[b * 8 + j] * scale + extra[j:j + 1, :]
        return 0

    lax.fori_loop(0, lat // 8, prepare, 0)
    pl.semaphore_wait(barrier, total - 1)

    lane = lax.broadcasted_iota(jnp.int32, (channels, 128), 1)

    def lat_copy(k, way):
        src = pl.ds(lat, 2) if way else pl.ds(2, 2)
        dst = pl.ds(0, 2) if way else pl.ds(lat + 2, 2)
        to = iy + 1 if way else iy - 1
        return pltpu.make_async_remote_copy(
            src_ref=basis.at[k, src], dst_ref=basis.at[k, dst], send_sem=lat_send.at[k, way],
            recv_sem=lat_recv.at[k, way], device_id=(ix, to), device_id_type=MESH)

    def lon_copy(k, way):
        return pltpu.make_async_remote_copy(
            src_ref=(east_out if way else west_out).at[k], dst_ref=(west_in if way else east_in).at[k],
            send_sem=lon_send.at[k, way], recv_sem=lon_recv.at[k, way],
            device_id=(east if way else west, iy), device_id_type=MESH)

    def send(k):
        @pl.when(iy < ny - 1)
        def _():
            lat_copy(k, 1).start()

        @pl.when(iy > 0)
        def _():
            lat_copy(k, 0).start()

        def pack(b, kept):
            to_west, to_east = kept
            for j in range(8):
                r = b * 8 + j
                here = (lane >= 2 * r) & (lane < 2 * r + 2)
                head = basis[k, r + 2, :, 0:128]
                tail = basis[k, r + 2, :, lon - 128:lon]
                to_west = jnp.where(here, pltpu.roll(head, 2 * r, 1), to_west)
                to_east = jnp.where(here, pltpu.roll(tail, lax.rem(2 * r + 2, 128), 1), to_east)
            return to_west, to_east

        empty = jnp.zeros((channels, 128), jnp.float32)
        to_west, to_east = lax.fori_loop(0, lat // 8, pack, (empty, empty))
        west_out[k] = to_west
        east_out[k] = to_east
        lon_copy(k, 0).start()
        lon_copy(k, 1).start()

    def dots(k):
        def one(i, _):
            def part(b, acc):
                acc = list(acc)
                for j in range(8):
                    r = b * 8 + j + 2
                    prod = basis[k, r] * basis[i, r]
                    n = 0
                    for h in range(channels // 8):
                        for t in range(tiles):
                            acc[n % 4] = acc[n % 4] + prod[8 * h:8 * h + 8, 128 * t:128 * t + 128]
                            n += 1
                return tuple(acc)

            zero = jnp.zeros((8, 128), jnp.float32)
            acc = lax.fori_loop(0, lat // 8, part, (zero,) * 4)
            gram_acc[lax.div(k * (k + 1), 2) + i] = (acc[0] + acc[1]) + (acc[2] + acc[3])
            return 0

        lax.fori_loop(0, k + 1, one, 0)

    def rows(k, b, theta):
        from_east, from_west = east_in[k], west_in[k]
        first = b * 8
        stack = jnp.concatenate([basis[k, first + 2 + j] for j in range(8)], axis=0)
        mixed = lax.dot_general(block[...], stack, (((1,), (0,)), ((), ())), precision=HI,
                                preferred_element_type=jnp.float32)
        planes = [coef[q, pl.ds(pl.multiple_of(first, 8), 8), :] for q in range(6)]
        for j in range(8):
            r = first + j
            x = [basis[k, r + 2, :, 128 * t:128 * t + 128] for t in range(tiles)]
            fwd1 = [pltpu.roll(v, 127, 1) for v in x] + [pltpu.roll(from_east, lax.rem(255 - 2 * r, 128), 1)]
            fwd2 = [pltpu.roll(v, 126, 1) for v in x] + [pltpu.roll(from_east, lax.rem(254 - 2 * r, 128), 1)]
            bwd1 = [pltpu.roll(from_west, lax.rem(255 - 2 * r, 128), 1)] + [pltpu.roll(v, 1, 1) for v in x]
            bwd2 = [pltpu.roll(from_west, lax.rem(256 - 2 * r, 128), 1)] + [pltpu.roll(v, 2, 1) for v in x]
            for t in range(tiles):
                cut = slice(128 * t, 128 * t + 128)
                e1 = jnp.where(lane < 127, fwd1[t], fwd1[t + 1])
                e2 = jnp.where(lane < 126, fwd2[t], fwd2[t + 1])
                w1 = jnp.where(lane >= 1, bwd1[t + 1], bwd1[t])
                w2 = jnp.where(lane >= 2, bwd2[t + 1], bwd2[t])

                def weight(q):
                    return planes[q][j:j + 1, cut]

                value = (diag[r, :, cut] - theta) * x[t] + mixed[channels * j:channels * (j + 1), cut]
                value = value + (weight(0) * e1 + weight(1) * w1 + weight(2) * (w2 - e2))
                value = value + (weight(3) * basis[k, r + 3, :, cut] + weight(4) * basis[k, r + 1, :, cut]
                                 + weight(5) * (basis[k, r, :, cut] - basis[k, r + 4, :, cut]))
                basis[k + 1, r + 2, :, cut] = value

    def step(k, _):
        theta = jnp.float32(THETA[0] * scale)
        for i in range(1, ITERS):
            theta = jnp.where(k == i, jnp.float32(THETA[i] * scale), theta)
        send(k)
        dots(k)
        lon_copy(k, 0).wait()
        lon_copy(k, 1).wait()

        def inner(b, _):
            rows(k, b, theta)
            return 0

        lax.fori_loop(1, lat // 8 - 1, inner, 0)

        @pl.when(iy < ny - 1)
        def _():
            lat_copy(k, 1).wait_send()
            lat_copy(k, 0).wait_recv()

        @pl.when(iy > 0)
        def _():
            lat_copy(k, 0).wait_send()
            lat_copy(k, 1).wait_recv()

        def outer(b, _):
            rows(k, b * (lat // 8 - 1), theta)
            return 0

        lax.fori_loop(0, 2, outer, 0)
        return 0

    lax.fori_loop(0, ITERS, step, 0)
    dots(ITERS)

    sums = jnp.concatenate(
        [jnp.sum(gram_acc[n], axis=0, keepdims=True) for n in range(len(PAIRS))]
        + [jnp.zeros((128 - len(PAIRS), 128), jnp.float32)], axis=0)
    flat = lax.dot_general(jnp.ones((8, 128), jnp.float32), sums, (((1,), (1,)), ((), ())), precision=HI,
                           preferred_element_type=jnp.float32)
    mine[...] = flat[0:1, :]
    slots[me] = flat[0:1, :]

    def share(o):
        other = lax.rem(me + o, total)
        return pltpu.make_async_remote_copy(
            src_ref=mine, dst_ref=slots.at[me], send_sem=red_send.at[o], recv_sem=red_recv.at[me],
            device_id=(other // ny, lax.rem(other, ny)), device_id_type=MESH)

    def take(o):
        other = lax.rem(me + total - o, total)
        return pltpu.make_async_remote_copy(
            src_ref=mine, dst_ref=slots.at[other], send_sem=red_send.at[o], recv_sem=red_recv.at[other],
            device_id=(other // ny, lax.rem(other, ny)), device_id_type=MESH)

    def give(o, _):
        share(o).start()
        return 0

    def get(o, _):
        take(o).wait_recv()
        share(o).wait_send()
        return 0

    lax.fori_loop(1, total, give, 0)
    lax.fori_loop(1, total, get, 0)
    whole = slots[0]
    for n in range(1, total):
        whole = whole + slots[n]
    gram = [[None] * (ITERS + 1) for _ in range(ITERS + 1)]
    for n, (k, i) in enumerate(PAIRS):
        gram[k][i] = gram[i][k] = jnp.broadcast_to(whole[:, n:n + 1], (8, 128))
    answer, applied = small_solve(gram)
    for k in range(ITERS):
        splats[k] = answer[k]
    for k in range(ITERS + 1):
        splats[ITERS + k] = applied[k]

    def finish(r, _):
        for h in range(channels // 8):
            for t in range(tiles):
                at = (slice(8 * h, 8 * h + 8), slice(128 * t, 128 * t + 128))
                x = basis[0, r + 2, at[0], at[1]]
                best = splats[0] * x
                rest = x - splats[ITERS] * x
                for k in range(1, ITERS + 1):
                    x = basis[k, r + 2, at[0], at[1]]
                    if k < ITERS:
                        best = best + splats[k] * x
                    rest = rest - splats[ITERS + k] * x
                outs[0, r, at[0], at[1]] = best
                outs[1, r, at[0], at[1]] = rest
        return 0

    lax.fori_loop(0, lat, finish, 0)
    stores = []
    for c in range(channels):
        for q, dst in enumerate((sol_hbm, res_hbm)):
            copy = pltpu.make_async_copy(outs.at[q, :, c, :], dst.at[c], out_sem.at[q, c])
            copy.start()
            stores.append(copy)
    for copy in stores:
        copy.wait()


def solution(mesh):
    nx, ny = mesh.shape["gx"], mesh.shape["gy"]

    def per_device(forcing, damping, coupling, wind_lon, wind_lat):
        channels, lat, lon = forcing.shape
        row_pos = (lax.axis_index("gy") * lat + jnp.arange(lat)).astype(jnp.float32)
        phi = -math.pi / 2 + (row_pos + 0.5) * (math.pi / (lat * ny))
        kx = (DIFF_LON / (jnp.cos(phi) ** 2 + 0.1))[:, None]
        f32 = jnp.float32
        vmem = pl.BlockSpec(memory_space=pltpu.VMEM)
        hbm = pl.BlockSpec(memory_space=pl.ANY)
        dma = pltpu.SemaphoreType.DMA
        shape = jax.ShapeDtypeStruct((channels, lat, lon), f32)
        return pl.pallas_call(
            functools.partial(kernel, nx, ny),
            out_shape=(shape, shape),
            in_specs=[hbm, hbm, vmem, vmem, vmem, vmem],
            out_specs=(hbm, hbm),
            scratch_shapes=[
                pltpu.VMEM((ITERS + 1, lat + 4, channels, lon), f32),
                pltpu.VMEM((lat, channels, lon), f32),
                pltpu.VMEM((7, lat, lon), f32),
                pltpu.VMEM((128, 128), f32),
                pltpu.VMEM((ITERS, channels, 128), f32),
                pltpu.VMEM((ITERS, channels, 128), f32),
                pltpu.VMEM((ITERS, channels, 128), f32),
                pltpu.VMEM((ITERS, channels, 128), f32),
                pltpu.VMEM((len(PAIRS), 8, 128), f32),
                pltpu.VMEM((1, 128), f32),
                pltpu.VMEM((nx * ny, 1, 128), f32),
                pltpu.VMEM((2 * ITERS + 1, 8, 128), f32),
                pltpu.VMEM((2, lat, channels, lon), f32),
                dma((2, channels)), dma((2, channels)),
                dma((ITERS, 2)), dma((ITERS, 2)), dma((ITERS, 2)), dma((ITERS, 2)),
                dma((nx * ny,)), dma((nx * ny,)),
            ],
            compiler_params=pltpu.CompilerParams(
                collective_id=0, has_side_effects=True, vmem_limit_bytes=40 * 1024 * 1024),
        )(forcing, damping, coupling, wind_lon, wind_lat, jnp.broadcast_to(kx, (lat, lon)))

    return jax.shard_map(
        per_device,
        mesh=mesh,
        in_specs=(P(None, "gy", "gx"), P(None, "gy", "gx"), P(), P("gy", "gx"), P("gy", "gx")),
        out_specs=(P(None, "gy", "gx"), P(None, "gy", "gx")),
        check_vma=False,
    )
```

time: 842 us -> 56.3 us (0.07); the launches traced: 828 us -> 56 us
  blocking collectives: 361 us -> 0 us
  between operations: 118 us -> 0.66 us
  other arithmetic: 98.6 us -> 0.05 us
  local copies, waits for them, and re-layouts: 99.7 us -> 5.13 us
  starting transfers between devices: 62.8 us -> 0 us
  waiting for transfers between devices: 57 us -> 0 us
  Pallas kernels: 0 us -> 50.1 us
  matrix products: 30.6 us -> 0 us
    psum x9 -> x0, blocking collectives: 361 us -> none  [the longest x8 319 us: per_device(): lax.psum((local_dots, jnp.sum(applied_in * applied_in)), ('gx', 'gy'))]
    ppermute x36 -> x0, starting transfers between devices: 62.8 us -> none  [the longest x18 43.8 us: with_halo(): lax.ppermute(tail, axis, [(i, (i + 1) % count) for i in range(ends)])]
    ppermute x36 -> x0, waiting for transfers between devices: 57 us -> none  [the longest x18 31.6 us: with_halo(): lax.ppermute(head, axis, [((i + 1) % count, i) for i in range(ends)])]
    pallas_call x0 -> x1, Pallas kernels: none -> 50.1 us  [per_device(): pl.pallas_call(functools.partial(kernel, nx, ny), out_shape=(shape, shape...]
    another operation x41 -> x0, other arithmetic: 48.4 us -> none
    slice x58 -> x0, local copies, waits for them, and re-layouts: 35.2 us -> none  [the longest x25 15.7 us: least_squares(): lower_val = column_vec[earlier + 1]]
    scatter x123 -> x0, local copies, waits for them, and re-layouts: 32.3 us -> none  [the longest x16 14.6 us: per_device(): heights.at[:column + 1, column].set(coeffs).at[column + 1, column]]
    dot_general x9 -> x0, matrix products: 30.6 us -> none  [apply_core(): jnp.einsum('ij,jab->iab', coupling, centre, precision=lax.Precision.HIGHEST)]
  transfers between devices with their start and end apart: 36 -> 0, of which waited for: 19 -> 0; matrix products, arithmetic and copies ran while one was open for 9% -> 0% of each run, Pallas kernels for 0% -> 0%
where the time goes in v1:
time: 56.3 us; the launch traced here: 56 us
  Pallas kernels  50.1 us (89%)
  local copies, waits for them, and re-layouts  5.13 us (9%)
  between operations  0.66 us (1%)
    pallas_call x1, Pallas kernels, per_device(): pl.pallas_call(functools.partial(kernel, nx, ny), out_shape=(shape, shape...  50.1 us
    unnamed x12, local copies, waits for them, and re-layouts  5.06 us

profile of v1, /device:TPU:0, one launch (start us, length us, event | category | flops | bytes accessed | tf_op | source)
XLA Modules:
  0.0 56.0 jit_solution(11174017299589718788)
XLA Ops:
  0.6 0.0 copy-start.2
  0.6 0.1 add_divide_fusion
  0.7 0.0 copy-start.4
  0.7 0.1 broadcast_in_dim.2.kx_ref
  0.8 0.6 %copy-done.2 = f32[32,256]{1,0:T(8,128)S(1)} copy-done((f32[32,256]{1,0:T(8,128)S(1)}, f32[32,256]{1,0:T(8,128)}, u32[]{:S(2)}) %copy-start.2) | copy-done | bytes 32792
  1.4 0.0 copy-done.4
  1.4 0.0 copy-start
  1.4 1.0 %copy-done = f32[16,32,256]{2,1,0:T(8,128)S(1)} copy-done((f32[16,32,256]{2,1,0:T(8,128)S(1)}, f32[16,32,256]{2,1,0:T(8,128)}, u32[]{:S(2)}) %copy-start) | copy-done | bytes 524312
  2.4 0.0 copy-start.1
  2.4 1.0 %copy-done.1 = f32[16,32,256]{2,1,0:T(8,128)S(1)} copy-done((f32[16,32,256]{2,1,0:T(8,128)S(1)}, f32[16,32,256]{2,1,0:T(8,128)}, u32[]{:S(2)}) %copy-start.1) | copy-done | bytes 524312
  3.5 0.0 copy-start.3
  3.5 0.8 %copy-done.3 = f32[32,256]{1,0:T(8,128)S(1)} copy-done((f32[32,256]{1,0:T(8,128)S(1)}, f32[32,256]{1,0:T(8,128)}, u32[]{:S(2)}) %copy-start.3) | copy-done | bytes 32792
  4.2 50.1 %shard_map.68 = (f32[16,32,256]{2,1,0:T(8,128)S(1)}, f32[16,32,256]{2,1,0:T(8,128)S(1)}) custom-call(f32[16,32,256]{2,1,0:T(8,128)S(1)} %copy-done, f32[16,32,256]{2,1,0:T(8,128)S(1)} %copy-done.1, f32[16,16]{1,0:T(8,128)S(1)} %copy-done.4, f32[32,256]{1,0:T(8,128)S(1)} %copy-done.2, f32[32,256]{1,0:T(8,128)S(1)} %copy-done.3, ...), custom_call_target="tpu_custom_call" | custom-call | tf_op jit(solution)/shard_map/pallas_call | solution.py:381
  54.4 0.8 %copy.9 = f32[16,32,256]{2,1,0:T(8,128)} copy(f32[16,32,256]{2,1,0:T(8,128)S(1)} %get-tuple-element.4) | data formatting | bytes 1048576
  55.2 0.8 %copy.10 = f32[16,32,256]{2,1,0:T(8,128)} copy(f32[16,32,256]{2,1,0:T(8,128)S(1)} %get-tuple-element.5) | data formatting | bytes 1048576
Async XLA Ops:
  0.6 0.8 %copy-start.2 = (f32[32,256]{1,0:T(8,128)S(1)}, f32[32,256]{1,0:T(8,128)}, u32[]{:S(2)}) copy-start(f32[32,256]{1,0:T(8,128)} %wl_ref.1) | copy-start | bytes 98308
  0.7 0.7 %copy-start.4 = (f32[16,16]{1,0:T(8,128)S(1)}, f32[16,16]{1,0:T(8,128)}, u32[]{:S(2)}) copy-start(f32[16,16]{1,0:T(8,128)} %c_ref.1) | copy-start | bytes 3076
  1.4 1.0 %copy-start = (f32[16,32,256]{2,1,0:T(8,128)S(1)}, f32[16,32,256]{2,1,0:T(8,128)}, u32[]{:S(2)}) copy-start(f32[16,32,256]{2,1,0:T(8,128)} %f_hbm.1) | copy-start | bytes 1572868
  2.4 1.0 %copy-start.1 = (f32[16,32,256]{2,1,0:T(8,128)S(1)}, f32[16,32,256]{2,1,0:T(8,128)}, u32[]{:S(2)}) copy-start(f32[16,32,256]{2,1,0:T(8,128)} %d_hbm.1) | copy-start | bytes 1572868
  3.5 0.8 %copy-start.3 = (f32[32,256]{1,0:T(8,128)S(1)}, f32[32,256]{1,0:T(8,128)}, u32[]{:S(2)}) copy-start(f32[32,256]{1,0:T(8,128)} %wa_ref.1) | copy-start | bytes 98308

commit v2 on v1

--- a/solution.py
+++ b/solution.py
@@ -21,7 +21,7 @@
 WIDTH = 3.0
 THETA = [MIDDLE + RADIUS * math.cos(math.pi * (2 * k + 1) / (2 * ITERS)) for k in (7, 0, 4, 2, 6, 1, 5, 3)]
 PAIRS = [(k, i) for k in range(ITERS + 1) for i in range(k + 1)]
-SLOTS = 48
+GROUP = 4
 
 
 def apply_to(coords):
@@ -90,9 +90,9 @@
     return answer, apply_to(answer)
 
 
-def kernel(nx, ny, f_hbm, d_hbm, c_ref, wl_ref, wa_ref, kx_ref, sol_hbm, res_hbm,
-           basis, diag, coef, block, west_in, east_in, west_out, east_out, gram_acc, mine, slots, splats, outs,
-           in_sem, out_sem, lat_send, lat_recv, lon_send, lon_recv, red_send, red_recv):
+def kernel(nx, ny, f_hbm, d_hbm, c_ref, wl_hbm, wa_hbm, kx_ref, sol_hbm, res_hbm,
+           basis, diag, coef, block, west_in, east_in, west_out, east_out, gram_acc, mine, slots, splats, outs, wl_ref, wa_ref,
+           in_sem, wind_sem, out_sem, lat_send, lat_recv, lon_send, lon_recv, red_send, red_recv):
     channels, lat, lon = f_hbm.shape
     tiles = lon // 128
     total = nx * ny
@@ -100,6 +100,9 @@
     me = ix * ny + iy
     east, west = lax.rem(ix + 1, nx), lax.rem(ix + nx - 1, nx)
 
+    winds = [pltpu.make_async_copy(wl_hbm, wl_ref, wind_sem.at[0]), pltpu.make_async_copy(wa_hbm, wa_ref, wind_sem.at[1])]
+    for copy in winds:
+        copy.start()
     loads = []
     for c in range(channels):
         for q, (src, dst) in enumerate(((f_hbm, basis.at[0]), (d_hbm, diag))):
@@ -118,52 +121,42 @@
     lax.fori_loop(1, total, greet, 0)
 
     scale = 1.0 / WIDTH
-    row = lax.broadcasted_iota(jnp.int32, (128, channels), 0)
-    col = lax.broadcasted_iota(jnp.int32, (128, channels), 1)
-    spread = jnp.where(lax.rem(row, channels) == col, 1.0, 0.0).astype(jnp.float32)
-    wide = lax.dot_general(spread, c_ref[...], (((1,), (0,)), ((), ())), precision=HI,
+    size = GROUP * channels
+
+    def spread(n):
+        row = lax.broadcasted_iota(jnp.int32, (n, channels), 0)
+        col = lax.broadcasted_iota(jnp.int32, (n, channels), 1)
+        return jnp.where(lax.rem(row, channels) == col, 1.0, 0.0).astype(jnp.float32)
+
+    wide = lax.dot_general(spread(size), c_ref[...], (((1,), (0,)), ((), ())), precision=HI,
                            preferred_element_type=jnp.float32)
-    wide = lax.dot_general(wide, spread, (((1,), (1,)), ((), ())), precision=HI,
-                           preferred_element_type=jnp.float32)
-    same = (lax.broadcasted_iota(jnp.int32, (128, 128), 0) // channels
-            == lax.broadcasted_iota(jnp.int32, (128, 128), 1) // channels)
-    block[...] = jnp.where(same, wide * (COUPLE * scale), 0.0)
+    wide = lax.dot_general(wide, spread(3 * size), (((1,), (1,)), ((), ())), precision=HI,
+                           preferred_element_type=jnp.float32) * (COUPLE * scale)
+    down = lax.broadcasted_iota(jnp.int32, (size, 3 * size), 0)
+    across = lax.broadcasted_iota(jnp.int32, (size, 3 * size), 1)
+    high = wide.astype(jnp.bfloat16).astype(jnp.float32)
+    wide = jnp.where(across < 2 * size, high, wide - high)
+    block[...] = jnp.where(down // channels == lax.rem(across, size) // channels, wide, 0.0).astype(jnp.bfloat16)
+    for copy in winds:
+        copy.wait()
     kx = kx_ref[...] * scale
     wl = wl_ref[...] * (scale / 12.0)
     wa = wa_ref[...] * (scale / 12.0)
-    coef[0] = 8.0 * wl - kx
-    coef[1] = -8.0 * wl - kx
-    coef[2] = wl
-    coef[3] = 8.0 * wa - DIFF_LAT * scale
-    coef[4] = -8.0 * wa - DIFF_LAT * scale
-    coef[5] = wa
-    coef[6] = 2.0 * kx + (1.0 + 2.0 * DIFF_LAT) * scale
-
-    def clear(k, _):
-        empty = jnp.zeros((2, channels, lon), jnp.float32)
-
-        @pl.when(iy == 0)
-        def _():
-            basis[k, 0:2] = empty
-
-        @pl.when(iy == ny - 1)
-        def _():
-            basis[k, lat + 2:lat + 4] = empty
-
-        return 0
-
-    lax.fori_loop(0, ITERS, clear, 0)
+    kx = jnp.concatenate([kx] * tiles, axis=1)
+    planes = (8.0 * wl - kx, -8.0 * wl - kx, wl, 8.0 * wa - DIFF_LAT * scale, -8.0 * wa - DIFF_LAT * scale, wa,
+              2.0 * kx + (1.0 + 2.0 * DIFF_LAT) * scale)
+    for q, plane in enumerate(planes):
+        for r in range(lat):
+            coef[r, q:q + 1, :] = plane[r:r + 1, :]
 
     for copy in loads:
         copy.wait()
 
-    def prepare(b, _):
-        extra = coef[6, pl.ds(pl.multiple_of(b * 8, 8), 8), :]
-        for j in range(8):
-            diag[b * 8 + j] = diag[b * 8 + j] * scale + extra[j:j + 1, :]
-        return 0
-
-    lax.fori_loop(0, lat // 8, prepare, 0)
+    def prepare(r, _):
+        diag[r] = diag[r] * scale + coef[r, 6:7, :]
+        return 0
+
+    lax.fori_loop(0, lat, prepare, 0)
     pl.semaphore_wait(barrier, total - 1)
 
     lane = lax.broadcasted_iota(jnp.int32, (channels, 128), 1)
@@ -182,7 +175,7 @@
             send_sem=lon_send.at[k, way], recv_sem=lon_recv.at[k, way],
             device_id=(east if way else west, iy), device_id_type=MESH)
 
-    def send(k):
+    def send_lat(k):
         @pl.when(iy < ny - 1)
         def _():
             lat_copy(k, 1).start()
@@ -191,19 +184,14 @@
         def _():
             lat_copy(k, 0).start()
 
-        def pack(b, kept):
-            to_west, to_east = kept
-            for j in range(8):
-                r = b * 8 + j
-                here = (lane >= 2 * r) & (lane < 2 * r + 2)
-                head = basis[k, r + 2, :, 0:128]
-                tail = basis[k, r + 2, :, lon - 128:lon]
-                to_west = jnp.where(here, pltpu.roll(head, 2 * r, 1), to_west)
-                to_east = jnp.where(here, pltpu.roll(tail, lax.rem(2 * r + 2, 128), 1), to_east)
-            return to_west, to_east
-
-        empty = jnp.zeros((channels, 128), jnp.float32)
-        to_west, to_east = lax.fori_loop(0, lat // 8, pack, (empty, empty))
+    def send_lon(k):
+        to_west = to_east = jnp.zeros((channels, 128), jnp.float32)
+        for r in range(lat):
+            here = (lane >= 2 * r) & (lane < 2 * r + 2)
+            head = basis[k, r + 2, :, 0:128]
+            tail = basis[k, r + 2, :, lon - 128:lon]
+            to_west = jnp.where(here, pltpu.roll(head, 2 * r, 1) if r else head, to_west)
+            to_east = jnp.where(here, pltpu.roll(tail, (2 * r + 2) % 128, 1), to_east)
         west_out[k] = to_west
         east_out[k] = to_east
         lon_copy(k, 0).start()
@@ -230,20 +218,19 @@
 
         lax.fori_loop(0, k + 1, one, 0)
 
-    def rows(k, b, theta):
+    def rows(k, picked, theta):
         from_east, from_west = east_in[k], west_in[k]
-        first = b * 8
-        stack = jnp.concatenate([basis[k, first + 2 + j] for j in range(8)], axis=0)
-        mixed = lax.dot_general(block[...], stack, (((1,), (0,)), ((), ())), precision=HI,
+        stack = jnp.concatenate([basis[k, r + 2] for r in picked], axis=0)
+        high = stack.astype(jnp.bfloat16)
+        low = (stack - high.astype(jnp.float32)).astype(jnp.bfloat16)
+        mixed = lax.dot_general(block[...], jnp.concatenate([high, low, high], axis=0), (((1,), (0,)), ((), ())),
                                 preferred_element_type=jnp.float32)
-        planes = [coef[q, pl.ds(pl.multiple_of(first, 8), 8), :] for q in range(6)]
-        for j in range(8):
-            r = first + j
+        for j, r in enumerate(picked):
             x = [basis[k, r + 2, :, 128 * t:128 * t + 128] for t in range(tiles)]
-            fwd1 = [pltpu.roll(v, 127, 1) for v in x] + [pltpu.roll(from_east, lax.rem(255 - 2 * r, 128), 1)]
-            fwd2 = [pltpu.roll(v, 126, 1) for v in x] + [pltpu.roll(from_east, lax.rem(254 - 2 * r, 128), 1)]
-            bwd1 = [pltpu.roll(from_west, lax.rem(255 - 2 * r, 128), 1)] + [pltpu.roll(v, 1, 1) for v in x]
-            bwd2 = [pltpu.roll(from_west, lax.rem(256 - 2 * r, 128), 1)] + [pltpu.roll(v, 2, 1) for v in x]
+            fwd1 = [pltpu.roll(v, 127, 1) for v in x] + [pltpu.roll(from_east, (255 - 2 * r) % 128, 1)]
+            fwd2 = [pltpu.roll(v, 126, 1) for v in x] + [pltpu.roll(from_east, (254 - 2 * r) % 128, 1)]
+            bwd1 = [pltpu.roll(from_west, (255 - 2 * r) % 128, 1)] + [pltpu.roll(v, 1, 1) for v in x]
+            bwd2 = [pltpu.roll(from_west, (256 - 2 * r) % 128, 1) if r % 64 else from_west] + [pltpu.roll(v, 2, 1) for v in x]
             for t in range(tiles):
                 cut = slice(128 * t, 128 * t + 128)
                 e1 = jnp.where(lane < 127, fwd1[t], fwd1[t + 1])
@@ -252,46 +239,70 @@
                 w2 = jnp.where(lane >= 2, bwd2[t + 1], bwd2[t])
 
                 def weight(q):
-                    return planes[q][j:j + 1, cut]
+                    return coef[r, q:q + 1, cut]
 
                 value = (diag[r, :, cut] - theta) * x[t] + mixed[channels * j:channels * (j + 1), cut]
                 value = value + (weight(0) * e1 + weight(1) * w1 + weight(2) * (w2 - e2))
-                value = value + (weight(3) * basis[k, r + 3, :, cut] + weight(4) * basis[k, r + 1, :, cut]
-                                 + weight(5) * (basis[k, r, :, cut] - basis[k, r + 4, :, cut]))
+                if r + 1 < lat:
+                    value = value + weight(3) * basis[k, r + 3, :, cut]
+                if r >= 1:
+                    value = value + weight(4) * basis[k, r + 1, :, cut]
+                south = basis[k, r, :, cut] if r >= 2 else None
+                north = basis[k, r + 4, :, cut] if r + 2 < lat else None
+                if south is None:
+                    value = value - weight(5) * north
+                elif north is None:
+                    value = value + weight(5) * south
+                else:
+                    value = value + weight(5) * (south - north)
                 basis[k + 1, r + 2, :, cut] = value
 
     def step(k, _):
         theta = jnp.float32(THETA[0] * scale)
         for i in range(1, ITERS):
             theta = jnp.where(k == i, jnp.float32(THETA[i] * scale), theta)
-        send(k)
         dots(k)
         lon_copy(k, 0).wait()
         lon_copy(k, 1).wait()
 
-        def inner(b, _):
-            rows(k, b, theta)
-            return 0
-
-        lax.fori_loop(1, lat // 8 - 1, inner, 0)
+        rows(k, (0, 1, lat - 2, lat - 1), theta)
+
+        @pl.when(iy > 0)
+        def _():
+            lat_copy(k, 1).wait_recv()
+            basis[k + 1, 2] += coef[0, 4:5, :] * basis[k, 1] + coef[0, 5:6, :] * basis[k, 0]
+            basis[k + 1, 3] += coef[1, 5:6, :] * basis[k, 1]
+
+            @pl.when(k + 1 < ITERS)
+            def _():
+                lat_copy(k + 1, 0).start()
+
+            lat_copy(k, 0).wait_send()
 
         @pl.when(iy < ny - 1)
         def _():
+            lat_copy(k, 0).wait_recv()
+            near = basis[k, lat + 2]
+            basis[k + 1, lat + 1] += coef[lat - 1, 3:4, :] * near - coef[lat - 1, 5:6, :] * basis[k, lat + 3]
+            basis[k + 1, lat] -= coef[lat - 2, 5:6, :] * near
+
+            @pl.when(k + 1 < ITERS)
+            def _():
+                lat_copy(k + 1, 1).start()
+
             lat_copy(k, 1).wait_send()
-            lat_copy(k, 0).wait_recv()
-
-        @pl.when(iy > 0)
+
+        for b in range((lat - 4) // GROUP):
+            rows(k, [2 + GROUP * b + j for j in range(GROUP)], theta)
+
+        @pl.when(k + 1 < ITERS)
         def _():
-            lat_copy(k, 0).wait_send()
-            lat_copy(k, 1).wait_recv()
-
-        def outer(b, _):
-            rows(k, b * (lat // 8 - 1), theta)
-            return 0
-
-        lax.fori_loop(0, 2, outer, 0)
-        return 0
-
+            send_lon(k + 1)
+
+        return 0
+
+    send_lat(0)
+    send_lon(0)
     lax.fori_loop(0, ITERS, step, 0)
     dots(ITERS)
 
@@ -381,13 +392,13 @@
         return pl.pallas_call(
             functools.partial(kernel, nx, ny),
             out_shape=(shape, shape),
-            in_specs=[hbm, hbm, vmem, vmem, vmem, vmem],
+            in_specs=[hbm, hbm, vmem, hbm, hbm, vmem],
             out_specs=(hbm, hbm),
             scratch_shapes=[
                 pltpu.VMEM((ITERS + 1, lat + 4, channels, lon), f32),
                 pltpu.VMEM((lat, channels, lon), f32),
-                pltpu.VMEM((7, lat, lon), f32),
-                pltpu.VMEM((128, 128), f32),
+                pltpu.VMEM((lat, 8, lon), f32),
+                pltpu.VMEM((GROUP * channels, 3 * GROUP * channels), jnp.bfloat16),
                 pltpu.VMEM((ITERS, channels, 128), f32),
                 pltpu.VMEM((ITERS, channels, 128), f32),
                 pltpu.VMEM((ITERS, channels, 128), f32),
@@ -397,13 +408,14 @@
                 pltpu.VMEM((nx * ny, 1, 128), f32),
                 pltpu.VMEM((2 * ITERS + 1, 8, 128), f32),
                 pltpu.VMEM((2, lat, channels, lon), f32),
-                dma((2, channels)), dma((2, channels)),
+                pltpu.VMEM((lat, lon), f32), pltpu.VMEM((lat, lon), f32),
+                dma((2, channels)), dma((2,)), dma((2, channels)),
                 dma((ITERS, 2)), dma((ITERS, 2)), dma((ITERS, 2)), dma((ITERS, 2)),
                 dma((nx * ny,)), dma((nx * ny,)),
             ],
             compiler_params=pltpu.CompilerParams(
-                collective_id=0, has_side_effects=True, vmem_limit_bytes=40 * 1024 * 1024),
-        )(forcing, damping, coupling, wind_lon, wind_lat, jnp.broadcast_to(kx, (lat, lon)))
+                collective_id=0, has_side_effects=True, vmem_limit_bytes=63 * 1024 * 1024),
+        )(forcing, damping, coupling, wind_lon, wind_lat, jnp.broadcast_to(kx, (lat, 128)))
 
     return jax.shard_map(
         per_device,

time: 56.3 us -> 50.3 us (0.89)
  Pallas kernels: 50.1 us -> 45.9 us
  local copies, waits for them, and re-layouts: 5.13 us -> 3.42 us
    pallas_call x1, Pallas kernels: 50.1 us -> 45.9 us  [per_device(): pl.pallas_call(functools.partial(kernel, nx, ny), out_shape=(shape, shape...]
    unnamed x12 -> x4, local copies, waits for them, and re-layouts: 5.06 us -> 2.74 us
    broadcast_in_dim x1, local copies, waits for them, and re-layouts: 0.07 us -> 0.69 us  [per_device(): jnp.broadcast_to(kx, (lat, 128))]
where the time goes in v2:
time: 50.3 us; the launch traced here: 50 us
  Pallas kernels  45.9 us (91%)
  local copies, waits for them, and re-layouts  3.42 us (7%)
  between operations  0.65 us (1%)
    pallas_call x1, Pallas kernels, per_device(): pl.pallas_call(functools.partial(kernel, nx, ny), out_shape=(shape, shape...  45.9 us
    unnamed x4, local copies, waits for them, and re-layouts  2.74 us

profile of v2, /device:TPU:0, one launch (start us, length us, event | category | flops | bytes accessed | tf_op | source)
XLA Modules:
  0.0 50.0 jit_solution(10308190727678890038)
XLA Ops:
  0.6 0.1 add_divide_fusion
  0.7 0.7 %broadcast_in_dim.2.kx_ref = f32[32,128]{1,0:T(8,128)} broadcast(f32[32]{0:T(128)S(1)} %add_divide_fusion), dimensions={0} | broadcast | bytes 16512 | tf_op jit(solution)/shard_map/broadcast_in_dim | solution.py:418
  1.4 45.9 %shard_map.68 = (f32[16,32,256]{2,1,0:T(8,128)}, f32[16,32,256]{2,1,0:T(8,128)}) custom-call(f32[16,32,256]{2,1,0:T(8,128)} %f_hbm.1, f32[16,32,256]{2,1,0:T(8,128)} %d_hbm.1, f32[16,16]{1,0:T(8,128)} %c_ref.1, f32[32,256]{1,0:T(8,128)} %wl_hbm.1, f32[32,256]{1,0:T(8,128)} %wa_hbm.1, f32[32,128]{1,0:T(8,128)} %broadcast_in_dim.2.kx_ref), custom_call_target="tpu_custom_call" | custom-call | tf_op jit(solution)/shard_map/pallas_call | solution.py:392
  47.3 0.0 copy-start
  47.3 1.9 %copy.9 = f32[16,32,256]{2,1,0:T(8,128)} copy(f32[16,32,256]{2,1,0:T(8,128)} %get-tuple-element.4) | data formatting | bytes 1048576
  49.2 0.0 copy-done
  49.2 0.8 %copy.10 = f32[16,32,256]{2,1,0:T(8,128)} copy(f32[16,32,256]{2,1,0:T(8,128)S(1)} %copy-done) | data formatting | bytes 1048576
Async XLA Ops:
  47.3 2.0 %copy-start = (f32[16,32,256]{2,1,0:T(8,128)S(1)}, f32[16,32,256]{2,1,0:T(8,128)}, u32[]{:S(2)}) copy-start(f32[16,32,256]{2,1,0:T(8,128)} %get-tuple-element.5) | copy-start | bytes 1572868

commit v3 on v2

--- a/solution.py
+++ b/solution.py
@@ -149,14 +149,9 @@
         for r in range(lat):
             coef[r, q:q + 1, :] = plane[r:r + 1, :]
 
-    for copy in loads:
+    for copy in loads[0::2]:
         copy.wait()
 
-    def prepare(r, _):
-        diag[r] = diag[r] * scale + coef[r, 6:7, :]
-        return 0
-
-    lax.fori_loop(0, lat, prepare, 0)
     pl.semaphore_wait(barrier, total - 1)
 
     lane = lax.broadcasted_iota(jnp.int32, (channels, 128), 1)
@@ -303,6 +298,14 @@
 
     send_lat(0)
     send_lon(0)
+    for copy in loads[1::2]:
+        copy.wait()
+
+    def prepare(r, _):
+        diag[r] = diag[r] * scale + coef[r, 6:7, :]
+        return 0
+
+    lax.fori_loop(0, lat, prepare, 0)
     lax.fori_loop(0, ITERS, step, 0)
     dots(ITERS)
 
@@ -349,31 +352,39 @@
     for k in range(ITERS + 1):
         splats[ITERS + k] = applied[k]
 
-    def finish(r, _):
-        for h in range(channels // 8):
-            for t in range(tiles):
-                at = (slice(8 * h, 8 * h + 8), slice(128 * t, 128 * t + 128))
-                x = basis[0, r + 2, at[0], at[1]]
-                best = splats[0] * x
-                rest = x - splats[ITERS] * x
-                for k in range(1, ITERS + 1):
-                    x = basis[k, r + 2, at[0], at[1]]
-                    if k < ITERS:
-                        best = best + splats[k] * x
-                    rest = rest - splats[ITERS + k] * x
-                outs[0, r, at[0], at[1]] = best
-                outs[1, r, at[0], at[1]] = rest
-        return 0
-
-    lax.fori_loop(0, lat, finish, 0)
-    stores = []
-    for c in range(channels):
-        for q, dst in enumerate((sol_hbm, res_hbm)):
-            copy = pltpu.make_async_copy(outs.at[q, :, c, :], dst.at[c], out_sem.at[q, c])
-            copy.start()
-            stores.append(copy)
-    for copy in stores:
-        copy.wait()
+    def store(q, c, b):
+        some = pl.ds(pl.multiple_of(b * 8, 8), 8)
+        return pltpu.make_async_copy(outs.at[q, some, c, :], (sol_hbm, res_hbm)[q].at[c, some, :], out_sem.at[q, c, b])
+
+    def finish(b, _):
+        for j in range(8):
+            r = b * 8 + j
+            for h in range(channels // 8):
+                for t in range(tiles):
+                    at = (slice(8 * h, 8 * h + 8), slice(128 * t, 128 * t + 128))
+                    x = basis[0, r + 2, at[0], at[1]]
+                    best = splats[0] * x
+                    rest = x - splats[ITERS] * x
+                    for k in range(1, ITERS + 1):
+                        x = basis[k, r + 2, at[0], at[1]]
+                        if k < ITERS:
+                            best = best + splats[k] * x
+                        rest = rest - splats[ITERS + k] * x
+                    outs[0, r, at[0], at[1]] = best
+                    outs[1, r, at[0], at[1]] = rest
+        for q in range(2):
+            for c in range(channels):
+                store(q, c, b).start()
+        return 0
+
+    def drain(b, _):
+        for q in range(2):
+            for c in range(channels):
+                store(q, c, b).wait()
+        return 0
+
+    lax.fori_loop(0, lat // 8, finish, 0)
+    lax.fori_loop(0, lat // 8, drain, 0)
 
 
 def solution(mesh):
@@ -409,7 +420,7 @@
                 pltpu.VMEM((2 * ITERS + 1, 8, 128), f32),
                 pltpu.VMEM((2, lat, channels, lon), f32),
                 pltpu.VMEM((lat, lon), f32), pltpu.VMEM((lat, lon), f32),
-                dma((2, channels)), dma((2,)), dma((2, channels)),
+                dma((2, channels)), dma((2,)), dma((2, channels, lat // 8)),
                 dma((ITERS, 2)), dma((ITERS, 2)), dma((ITERS, 2)), dma((ITERS, 2)),
                 dma((nx * ny,)), dma((nx * ny,)),
             ],

time: 50.3 us -> 51.1 us (1.016)
  Pallas kernels: 45.9 us -> 46.7 us
    pallas_call x1, Pallas kernels: 45.9 us -> 46.7 us  [per_device(): pl.pallas_call(functools.partial(kernel, nx, ny), out_shape=(shape, shape...]
where the time goes in v3:
time: 51.1 us; the launch traced here: 50.8 us
  Pallas kernels  46.7 us (91%)
  local copies, waits for them, and re-layouts  3.42 us (7%)
  between operations  0.65 us (1%)
    pallas_call x1, Pallas kernels, per_device(): pl.pallas_call(functools.partial(kernel, nx, ny), out_shape=(shape, shape...  46.7 us
    unnamed x4, local copies, waits for them, and re-layouts  2.74 us

profile of v3, /device:TPU:0, one launch (start us, length us, event | category | flops | bytes accessed | tf_op | source)
XLA Modules:
  0.0 50.8 jit_solution(12784543162710180417)
XLA Ops:
  0.6 0.1 add_divide_fusion
  0.7 0.7 %broadcast_in_dim.2.kx_ref = f32[32,128]{1,0:T(8,128)} broadcast(f32[32]{0:T(128)S(1)} %add_divide_fusion), dimensions={0} | broadcast | bytes 16512 | tf_op jit(solution)/shard_map/broadcast_in_dim | solution.py:429
  1.4 46.7 %shard_map.68 = (f32[16,32,256]{2,1,0:T(8,128)}, f32[16,32,256]{2,1,0:T(8,128)}) custom-call(f32[16,32,256]{2,1,0:T(8,128)} %f_hbm.1, f32[16,32,256]{2,1,0:T(8,128)} %d_hbm.1, f32[16,16]{1,0:T(8,128)} %c_ref.1, f32[32,256]{1,0:T(8,128)} %wl_hbm.1, f32[32,256]{1,0:T(8,128)} %wa_hbm.1, f32[32,128]{1,0:T(8,128)} %broadcast_in_dim.2.kx_ref), custom_call_target="tpu_custom_call" | custom-call | tf_op jit(solution)/shard_map/pallas_call | solution.py:403
  48.0 0.0 copy-start
  48.1 1.9 %copy.9 = f32[16,32,256]{2,1,0:T(8,128)} copy(f32[16,32,256]{2,1,0:T(8,128)} %get-tuple-element.4) | data formatting | bytes 1048576
  50.0 0.0 copy-done
  50.0 0.8 %copy.10 = f32[16,32,256]{2,1,0:T(8,128)} copy(f32[16,32,256]{2,1,0:T(8,128)S(1)} %copy-done) | data formatting | bytes 1048576
Async XLA Ops:
  48.0 2.0 %copy-start = (f32[16,32,256]{2,1,0:T(8,128)S(1)}, f32[16,32,256]{2,1,0:T(8,128)}, u32[]{:S(2)}) copy-start(f32[16,32,256]{2,1,0:T(8,128)} %get-tuple-element.5) | copy-start | bytes 1572868
